TPU v7x, 256 devices: a whole 4x4x8 slice. The times are simulated.
256 devices in a mesh: dp: 64 (over z, x, core), rep: 4 (over y).
Axes of the slice: x: 4, y: 4, z: 8, core: 2. Of those that a mesh axis runs over, the one named last changes fastest.
Arguments:
- tokens: bfloat16 [65536, 2048], P(('rep', 'dp')), parts along dimension 0, may hold values from -12 to 12
- router: bfloat16 [8192, 64], P('rep'), parts along dimension 0, may hold values from -12 to 12
- w_gate: bfloat16 [64, 2048, 768], P('dp'), may hold values from -0.125 to 0.125
- w_up: bfloat16 [64, 2048, 768], P('dp'), may hold values from -0.125 to 0.125
- w_down: bfloat16 [64, 768, 2048], P('dp'), may hold values from -0.21875 to 0.21875
- picks: int32 [256, 256], P(('rep', 'dp')), parts along dimension 0, may hold values from 0 to 16383, as said below
Outputs:
- combined: bfloat16 [65536, 2048], P(('rep', 'dp')), parts along dimension 0
There are 4 independent parts, one for each index of `rep`. A program takes and returns all parts, laid end to end along the dimension named above; an argument that names none is the same for every part. Nothing has to cross between parts.
Inputs may be any that keep to these rules, and one draw needn't show every extreme that they name: `picks`: row e holds 256 different tokens taken by expert e, sorted by the device that holds them (256 tokens each, in order); at most 6 of them lie among one device's tokens, and in every row exactly 6 lie among some device's tokens.
All inputs are finite; a program needn't handle non-finite values.
Results may differ from a plain program's by a relative error of at most 0.0062.
Values may be sent and summed in bfloat16 or wider, within the bound.
A program may use at most 64 MiB of HBM per device.

v0:
```python
import jax
import jax.numpy as jnp
from jax import lax
from jax.sharding import PartitionSpec as P

MOST = 6


def feed_forward(buffer_rows, gate_values, gate_w, up_w, down_w):
    gate_act = jnp.dot(buffer_rows, gate_w, preferred_element_type=jnp.float32)
    up_act = jnp.dot(buffer_rows, up_w, preferred_element_type=jnp.float32)
    hidden = (gate_values.astype(jnp.float32)[:, None] * jax.nn.silu(gate_act) * up_act).astype(
        jnp.bfloat16
    )
    return jnp.dot(hidden, down_w, preferred_element_type=jnp.float32).astype(jnp.bfloat16)


def body(tokens, router, w_gate, w_up, w_down, picks):
    sources = lax.axis_size("dp")
    tok_dev = tokens.shape[0]
    width = tokens.shape[1]
    experts = router.shape[1]
    my_picks = picks[0]
    capacity = my_picks.shape[0]
    logits = jnp.dot(tokens, router, preferred_element_type=jnp.float32)
    shares = jax.nn.softmax(logits, axis=1)
    source_of = my_picks // tok_dev
    block_ids = jnp.arange(sources, dtype=jnp.int32)
    counts = jnp.sum((source_of[None, :] == block_ids[:, None]).astype(jnp.int32), axis=1)
    starts = jnp.cumsum(counts) - counts
    slot_pos = jnp.arange(MOST, dtype=jnp.int32)
    within = jnp.arange(capacity, dtype=jnp.int32) - starts[source_of]
    flat_index = source_of * MOST + within
    position = jnp.clip(starts[:, None] + slot_pos[None, :], 0, capacity - 1)
    to_owner = jnp.where(
        slot_pos[None, :] < counts[:, None], my_picks[position] - block_ids[:, None] * tok_dev, -1
    )
    local_index = lax.all_to_all(to_owner, "dp", split_axis=0, concat_axis=0, tiled=True)
    live_slot = local_index >= 0
    safe_index = jnp.maximum(local_index, 0)
    send_rows = jnp.where(live_slot[:, :, None], tokens[safe_index], jnp.zeros((), tokens.dtype))
    columns = lax.all_to_all(
        shares.T.astype(jnp.bfloat16), "dp", split_axis=0, concat_axis=1, tiled=True
    ).astype(jnp.float32)
    gate_dense = (experts * columns[0][my_picks]).astype(jnp.bfloat16)
    received = lax.all_to_all(send_rows, "dp", split_axis=0, concat_axis=0, tiled=True)
    gate_flat = jnp.zeros((sources * MOST,), jnp.bfloat16).at[flat_index].set(gate_dense)
    buffer_rows = received.reshape(sources * MOST, width)
    expert_out = feed_forward(buffer_rows, gate_flat, w_gate[0], w_up[0], w_down[0])
    returned = lax.all_to_all(
        expert_out.reshape(sources, MOST, width), "dp", split_axis=0, concat_axis=0, tiled=True
    )
    onehot = (local_index.reshape(1, -1) == jnp.arange(tok_dev, dtype=jnp.int32)[:, None]).astype(
        jnp.bfloat16
    )
    combined = jnp.dot(
        onehot, returned.reshape(sources * MOST, width), preferred_element_type=jnp.float32
    )
    return combined.astype(jnp.bfloat16)


def solution(mesh):
    return jax.shard_map(
        body,
        mesh=mesh,
        in_specs=(
            P(("rep", "dp"), None),
            P("rep", None),
            P("dp", None, None),
            P("dp", None, None),
            P("dp", None, None),
            P(("rep", "dp"), None),
        ),
        out_specs=P(("rep", "dp"), None),
        check_vma=False,
    )
```

profile of v0, /device:TPU:55, one launch (start us, length us, event | category | flops | bytes accessed | tf_op | source)
XLA Modules:
  0.0 187.6 jit_solution(8847566476358360242)
XLA Ops:
  0.0 0.8 and_select_fusion.1
  1.6 2.8 %gather_fusion = s32[384]{0:T(512)S(1)} fusion(s32[256]{0:T(256)S(1)} %bitcast.52, s32[1024]{0:T(1024)S(1)} %pad_clamp_fusion.3), kind=kCustom, calls=%fused_computation | custom fusion | bytes 4608 | tf_op jit(solution)/shard_map/gather | solution.py:36
  4.5 0.7 subtract_select_fusion
  5.2 11.8 %all-to-all-start = ((s32[64,1,6]{2,1,0:T(1,128)}), s32[64,1,6]{2,1,0:T(1,128)S(1)}, u32[]{:S(2)}, u32[]{:S(2)}) async-start(s32[64,1,6]{2,1,0:T(1,128)} %bitcast.3), calls=%async_computation | async-start | bytes 65536 | tf_op jit(solution)/shard_map/all_to_all | solution.py:38
  17.0 1.7 fusion.25
  20.7 3.0 %all-to-all-done = s32[64,1,6]{2,1,0:T(1,128)S(1)} async-done(((s32[64,1,6]{2,1,0:T(1,128)}), s32[64,1,6]{2,1,0:T(1,128)S(1)}, u32[]{:S(2)}, u32[]{:S(2)}) %all-to-all-start) | async-done | bytes 1568 | tf_op jit(solution)/shard_map/all_to_all | solution.py:38
  23.7 7.5 %all-to-all-start.1 = ((bf16[64,2,128]{2,1,0:T(2,128)(2,1)}), bf16[64,2,128]{2,1,0:T(2,128)(2,1)S(1)}, u32[]{:S(2)}, u32[]{:S(2)}) async-start(bf16[64,2,128]{2,1,0:T(2,128)(2,1)} %reshape.373), calls=%async_computation.1 | async-start | bytes 65536 | tf_op jit(solution)/shard_map/all_to_all | solution.py:42
  31.6 6.4 %gather_fusion.3 = bf16[384,2048]{1,0:T(8,128)(2,1)} fusion(bf16[256,2048]{1,0:T(8,128)(2,1)} %param.6, s32[1024]{0:T(1024)S(1)} %pad_clamp_fusion), kind=kCustom, calls=%fused_computation.3 | custom fusion | bytes 3147264 | tf_op jit(solution)/shard_map/gather | solution.py:41
  38.0 3.7 %reshape.342 = bf16[64,6,2048]{2,1,0:T(8,128)(2,1)} reshape(bf16[384,2048]{1,0:T(8,128)(2,1)} %gather_fusion.3) | data formatting | bytes 3145728 | tf_op jit(solution)/shard_map/gather | solution.py:41
  41.7 3.1 %broadcast_select_fusion = bf16[64,6,2048]{2,1,0:T(8,128)(2,1)} fusion(bf16[64,6,2048]{2,1,0:T(8,128)(2,1)} %reshape.342, pred[64,6]{1,0:T(8,128)(4,1)S(1)} %copy.23), kind=kLoop, calls=%fused_computation.13 | loop fusion | flops 786432 | bytes 3146112 | tf_op jit(solution)/shard_map/jit(_where)/select_n | solution.py:41
  44.8 10.5 %all-to-all-start.2 = ((bf16[64,6,2048]{2,1,0:T(8,128)(2,1)}), bf16[64,6,2048]{2,1,0:T(8,128)(2,1)}, u32[]{:S(2)}, u32[]{:S(2)}) async-start(bf16[64,6,2048]{2,1,0:T(8,128)(2,1)} %broadcast_select_fusion), calls=%async_computation.2 | async-start | bytes 4194304 | tf_op jit(solution)/shard_map/all_to_all | solution.py:46
  55.4 1.9 gather_fusion.1
  57.4 1.7 gather_fusion.2
  59.1 2.3 %scatter_custom_fusion = bf16[384]{0:T(512)(128)(2,1)S(1)} fusion(s32[256]{0:T(256)S(1)} %bitcast.58, bf16[256]{0:T(256)(128)(2,1)S(1)} %multiply_convert_fusion, bf16[]{:T(256)} %constant.13.clone.1), kind=kCustom, calls=%fused_computation.48 | custom fusion | bytes 770 | tf_op jit(solution)/shard_map/scatter | solution.py:47
  61.5 43.5 %all-to-all-done.2 = bf16[64,6,2048]{2,1,0:T(8,128)(2,1)} async-done(((bf16[64,6,2048]{2,1,0:T(8,128)(2,1)}), bf16[64,6,2048]{2,1,0:T(8,128)(2,1)}, u32[]{:S(2)}, u32[]{:S(2)}) %all-to-all-start.2) | async-done | bytes 1572896 | tf_op jit(solution)/shard_map/all_to_all | solution.py:46
  105.0 3.7 %reshape.313 = bf16[384,2048]{1,0:T(8,128)(2,1)} reshape(bf16[64,6,2048]{2,1,0:T(8,128)(2,1)} %all-to-all-done.2) | data formatting | bytes 3145728 | tf_op jit(solution)/shard_map/reshape | solution.py:48
  108.7 4.8 %fusion.4 = f32[384,768]{1,0:T(8,128)} fusion(bf16[384,2048]{1,0:T(8,128)(2,1)} %reshape.313, bf16[1,2048,768]{2,1,0:T(8,128)(2,1)} %param.8), kind=kOutput, calls=%fused_computation.9 | convolution fusion | flops 1207959552 | bytes 5898240 | tf_op jit(solution)/shard_map/dot_general | solution.py:10
  113.5 6.9 %fusion.6 = bf16[384,2048]{1,0:T(8,128)(2,1)} fusion(bf16[1,768,2048]{2,1,0:T(8,128)(2,1)S(1)} %copy-done, bf16[384,2048]{1,0:T(8,128)(2,1)} %reshape.313, bf16[1,2048,768]{2,1,0:T(8,128)(2,1)} %param.9, f32[384,768]{1,0:T(8,128)} %fusion.4, f32[384]{0:T(512)S(1)} %convert_element_type.40), kind=kOutput, calls=%fused_computation.11 | convolution fusion | flops 2418769920 | bytes 10618368 | tf_op jit(solution)/shard_map/dot_general | solution.py:15
  120.4 3.7 %reshape.314 = bf16[64,6,2048]{2,1,0:T(8,128)(2,1)} reshape(bf16[384,2048]{1,0:T(8,128)(2,1)} %fusion.6) | data formatting | bytes 3145728 | tf_op jit(solution)/shard_map/reshape | solution.py:51
  124.1 7.1 %all-to-all-start.3 = ((bf16[64,6,2048]{2,1,0:T(8,128)(2,1)}), bf16[64,6,2048]{2,1,0:T(8,128)(2,1)}, u32[]{:S(2)}, u32[]{:S(2)}) async-start(bf16[64,6,2048]{2,1,0:T(8,128)(2,1)} %reshape.314), calls=%async_computation.3 | async-start | bytes 4194304 | tf_op jit(solution)/shard_map/all_to_all | solution.py:50
  131.7 0.7 reduce.4
  132.6 48.3 %all-to-all-done.3 = bf16[64,6,2048]{2,1,0:T(8,128)(2,1)} async-done(((bf16[64,6,2048]{2,1,0:T(8,128)(2,1)}), bf16[64,6,2048]{2,1,0:T(8,128)(2,1)}, u32[]{:S(2)}, u32[]{:S(2)}) %all-to-all-start.3) | async-done | bytes 1572896 | tf_op jit(solution)/shard_map/all_to_all | solution.py:50
  180.8 3.7 %reshape.315 = bf16[384,2048]{1,0:T(8,128)(2,1)} reshape(bf16[64,6,2048]{2,1,0:T(8,128)(2,1)} %all-to-all-done.3) | data formatting | bytes 3145728 | tf_op jit(solution)/shard_map/reshape | solution.py:57
  184.5 3.1 %convolution_convert_fusion = bf16[256,2048]{1,0:T(8,128)(2,1)} fusion(bf16[384,2048]{1,0:T(8,128)(2,1)} %reshape.315, s32[384]{0:T(512)S(1)} %eq.34), kind=kOutput, calls=%fused_computation.12 | convolution fusion | flops 403275776 | bytes 2622976 | tf_op jit(solution)/shard_map/dot_general | solution.py:56
  (39 shorter events, 4.0 us)
Async XLA Ops:
  0.0 113.5 %copy-start = (bf16[1,768,2048]{2,1,0:T(8,128)(2,1)S(1)}, bf16[1,768,2048]{2,1,0:T(8,128)(2,1)}, u32[]{:S(2)}) copy-start(bf16[1,768,2048]{2,1,0:T(8,128)(2,1)} %param.10) | copy-start | bytes 9437188
  0.0 1.5 copy-start.1
  1.5 15.5 %copy-start.2 = (bf16[2048,64]{0,1:T(8,128)(2,1)S(1)}, bf16[2048,64]{0,1:T(8,128)(2,1)}, u32[]{:S(2)}) copy-start(bf16[2048,64]{0,1:T(8,128)(2,1)} %param.7) | copy-start | bytes 786436
  5.2 18.4 %all-to-all-start = ((s32[64,1,6]{2,1,0:T(1,128)}), s32[64,1,6]{2,1,0:T(1,128)S(1)}, u32[]{:S(2)}, u32[]{:S(2)}) async-start(s32[64,1,6]{2,1,0:T(1,128)} %bitcast.3), calls=%async_computation | async-start | bytes 65536 | tf_op jit(solution)/shard_map/all_to_all | solution.py:38
  23.7 21.2 %all-to-all-start.1 = ((bf16[64,2,128]{2,1,0:T(2,128)(2,1)}), bf16[64,2,128]{2,1,0:T(2,128)(2,1)S(1)}, u32[]{:S(2)}, u32[]{:S(2)}) async-start(bf16[64,2,128]{2,1,0:T(2,128)(2,1)} %reshape.373), calls=%async_computation.1 | async-start | bytes 65536 | tf_op jit(solution)/shard_map/all_to_all | solution.py:42
  44.8 60.2 %all-to-all-start.2 = ((bf16[64,6,2048]{2,1,0:T(8,128)(2,1)}), bf16[64,6,2048]{2,1,0:T(8,128)(2,1)}, u32[]{:S(2)}, u32[]{:S(2)}) async-start(bf16[64,6,2048]{2,1,0:T(8,128)(2,1)} %broadcast_select_fusion), calls=%async_computation.2 | async-start | bytes 4194304 | tf_op jit(solution)/shard_map/all_to_all | solution.py:46
  124.1 56.8 %all-to-all-start.3 = ((bf16[64,6,2048]{2,1,0:T(8,128)(2,1)}), bf16[64,6,2048]{2,1,0:T(8,128)(2,1)}, u32[]{:S(2)}, u32[]{:S(2)}) async-start(bf16[64,6,2048]{2,1,0:T(8,128)(2,1)} %reshape.314), calls=%async_computation.3 | async-start | bytes 4194304 | tf_op jit(solution)/shard_map/all_to_all | solution.py:50
where the time goes:
time: 190 us; the launch traced here: 188 us
  waiting for transfers between devices  94.8 us (50%)
  starting transfers between devices  36.9 us (19%)
  local copies, waits for them, and re-layouts  32.6 us (17%)
  matrix products  16.4 us (9%)
  other arithmetic  6.72 us (4%)
    all_to_all x1, waiting for transfers between devices, body(): lax.all_to_all(expert_out.reshape(sources, MOST, width), 'dp', split_axis...  48.3 us
    all_to_all x1, waiting for transfers between devices, body(): lax.all_to_all(send_rows, 'dp', split_axis=0, concat_axis=0, tiled=True)  43.5 us
    all_to_all x1, starting transfers between devices, body(): lax.all_to_all(to_owner, 'dp', split_axis=0, concat_axis=0, tiled=True)  11.8 us
    all_to_all x1, starting transfers between devices, body(): lax.all_to_all(send_rows, 'dp', split_axis=0, concat_axis=0, tiled=True)  10.5 us
    gather x2, local copies, waits for them, and re-layouts, body(): tokens[safe_index]  10.1 us
    all_to_all x1, starting transfers between devices, body(): lax.all_to_all(shares.T.astype(jnp.bfloat16), 'dp', split_axis=0, concat_...  7.46 us
    all_to_all x1, starting transfers between devices, body(): lax.all_to_all(expert_out.reshape(sources, MOST, width), 'dp', split_axis...  7.1 us
    dot_general x1, matrix products, feed_forward(): jnp.dot(hidden, down_w, preferred_element_type=jnp.float32)  6.88 us
  transfers between devices with their start and end apart: 4, of which 3 were waited for; matrix products, arithmetic and copies ran while one was open for 13% of the time, Pallas kernels for 0%

commit v1 on v0

v1 whole, which is shorter than its diff:
```python
import functools

import jax
import jax.numpy as jnp
from jax import lax
from jax.experimental import pallas as pl
from jax.experimental.pallas import tpu as pltpu
from jax.sharding import PartitionSpec as P

MOST = 6
PLANE = 8
SUB, LANE = 16, 128
MESH = pl.DeviceIdType.MESH


def swap_matrix():
    row = lax.broadcasted_iota(jnp.int32, (SUB * SUB, SUB * SUB), 0)
    col = lax.broadcasted_iota(jnp.int32, (SUB * SUB, SUB * SUB), 1)
    swapped = (col % SUB) * SUB + col // SUB
    return (row == swapped).astype(jnp.float32).astype(jnp.bfloat16)


def swap(matrix, stacked):
    return jnp.dot(matrix, stacked, preferred_element_type=jnp.float32).astype(jnp.bfloat16)


def plane_tiles(buffer, plane, part):
    tiles = [
        buffer[plane * PLANE + member, 2 * part + half]
        for half in range(2)
        for member in range(PLANE)
    ]
    return jnp.concatenate(tiles, axis=0)


def to_rows(matrix, buffer, planes, target, target_row):
    jobs = [(plane, part) for plane in planes for part in range(MOST // 2)]
    for first in range(0, len(jobs), 2):
        pair = jobs[first : first + 2]
        stacked = jnp.concatenate([plane_tiles(buffer, *job) for job in pair], axis=1)
        moved = swap(matrix, stacked)
        for which in range(len(pair)):
            at = target_row + (first + which) * SUB
            for chunk in range(SUB):
                target[pl.ds(at, SUB), chunk * LANE : (chunk + 1) * LANE] = moved[
                    chunk * SUB : (chunk + 1) * SUB, which * LANE : (which + 1) * LANE
                ]


def to_tiles(matrix, rows, first_row):
    def stack(at):
        return jnp.concatenate(
            [rows[pl.ds(at, SUB), chunk * LANE : (chunk + 1) * LANE] for chunk in range(SUB)],
            axis=0,
        )

    stacked = jnp.concatenate([stack(first_row), stack(first_row + SUB)], axis=1)
    moved = swap(matrix, stacked)
    return [
        moved[row * SUB : (row + 1) * SUB, half * LANE : (half + 1) * LANE]
        for half in range(2)
        for row in range(SUB)
    ]


def kernel(
    n,
    tokens_hbm,
    router_hbm,
    gate_hbm,
    up_hbm,
    down_hbm,
    picks_ref,
    out_ref,
    tokens,
    router,
    gate_w,
    up_w,
    down_w,
    token_tiles,
    gates_t,
    all_picks,
    slots_v,
    slots_s,
    mix_t,
    mix,
    send_buf,
    recv_buf,
    rows,
    hidden,
    result_rows,
    result_buf,
    return_buf,
    return_rows,
    load_sem,
    slot_sem,
    local_sem,
    pick_send,
    pick_recv,
    row_send,
    row_recv,
    result_send,
    result_recv,
):
    me = lax.axis_index("dp")
    planes = n // PLANE
    my_plane = me // PLANE
    tok_dev, width = tokens.shape
    capacity = picks_ref.shape[1]
    steps = planes // 2

    def step_planes(step):
        up = step + 1
        down = jnp.where(step == steps - 1, 0, planes - 1 - step)
        return lax.rem(my_plane + up, planes), lax.rem(my_plane + down, planes)

    loads = [
        pltpu.make_async_copy(tokens_hbm, tokens, load_sem.at[0]),
        pltpu.make_async_copy(router_hbm, router, load_sem.at[1]),
        pltpu.make_async_copy(gate_hbm.at[0], gate_w, load_sem.at[2]),
        pltpu.make_async_copy(up_hbm.at[0], up_w, load_sem.at[3]),
        pltpu.make_async_copy(down_hbm.at[0], down_w, load_sem.at[4]),
    ]
    for load in loads:
        load.start()

    barrier = pltpu.get_barrier_semaphore()

    @pl.loop(1, n)
    def _(shift):
        pl.semaphore_signal(
            barrier, inc=1, device_id={"dp": lax.rem(me + shift, n)}, device_id_type=MESH
        )

    pl.semaphore_wait(barrier, n - 1)

    def pick_copy(target):
        return pltpu.make_async_remote_copy(
            src_ref=picks_ref,
            dst_ref=all_picks.at[me],
            send_sem=pick_send,
            recv_sem=pick_recv.at[my_plane],
            device_id={"dp": target},
            device_id_type=MESH,
        )

    @pl.loop(0, steps)
    def _(step):
        for plane in step_planes(step):

            @pl.loop(0, PLANE)
            def _(member):
                target = plane * PLANE + member

                @pl.when(target != me)
                def _():
                    pick_copy(target).start()

    all_picks[me] = picks_ref[...]

    matrix = swap_matrix()
    loads[0].wait()
    loads[1].wait()
    logits = jnp.dot(tokens[...], router[...], preferred_element_type=jnp.float32)
    logits = logits.T
    powers = jnp.exp(logits - jnp.max(logits, axis=0, keepdims=True))
    shares = powers / jnp.sum(powers, axis=0, keepdims=True)
    gates_t[...] = (n * shares).astype(jnp.bfloat16).astype(jnp.float32)

    @pl.loop(0, tok_dev // (2 * SUB))
    def _(block):
        at = pl.multiple_of(block * 2 * SUB, 2 * SUB)
        tiles = to_tiles(matrix, tokens, at)
        for index, tile in enumerate(tiles):
            token_tiles[at + index] = tile

    token_tiles[tok_dev] = jnp.zeros((SUB, LANE), jnp.bfloat16)

    def row_copy(target):
        return pltpu.make_async_remote_copy(
            src_ref=send_buf.at[target],
            dst_ref=recv_buf.at[me],
            send_sem=row_send,
            recv_sem=row_recv.at[my_plane],
            device_id={"dp": target},
            device_id_type=MESH,
        )

    def result_copy(target):
        return pltpu.make_async_remote_copy(
            src_ref=result_buf.at[target],
            dst_ref=return_buf.at[me],
            send_sem=result_send,
            recv_sem=result_recv.at[my_plane],
            device_id={"dp": target},
            device_id_type=MESH,
        )

    own_rows = pltpu.make_async_copy(send_buf.at[me], recv_buf.at[me], local_sem.at[0])
    own_results = pltpu.make_async_copy(result_buf.at[me], return_buf.at[me], local_sem.at[1])

    def send_plane(plane, copy, own):
        @pl.loop(0, PLANE)
        def _(member):
            target = plane * PLANE + member

            @pl.when(target != me)
            def _():
                copy(target).start()

            @pl.when(target == me)
            def _():
                own.start()

    def wait_plane(plane, buffer, semaphores, own):
        @pl.when(plane != my_plane)
        def _():
            part = buffer.at[pl.ds(plane * PLANE, PLANE)]
            pltpu.make_async_copy(part, part, semaphores.at[plane]).wait()

        @pl.when(plane == my_plane)
        def _():
            part = buffer.at[pl.ds(plane * PLANE, PLANE - 1)]
            pltpu.make_async_copy(part, part, semaphores.at[plane]).wait()
            if own is not None:
                own.wait()

    lane = lax.broadcasted_iota(jnp.int32, (PLANE, capacity), 1)
    token_lane = lax.broadcasted_iota(jnp.int32, (PLANE, tok_dev), 1)
    slot_lane = lax.broadcasted_iota(jnp.int32, (PLANE, LANE), 1)

    @pl.loop(0, steps)
    def _(step):
        for plane in step_planes(step):
            wait_plane(plane, all_picks, pick_recv, None)
            first = pl.multiple_of(plane * PLANE, PLANE)
            picked = all_picks[pl.ds(first, PLANE)].reshape(PLANE, capacity)
            local = picked - me * tok_dev
            mine = (local >= 0) & (local < tok_dev)
            before = jnp.sum((local < 0).astype(jnp.int32), axis=1, keepdims=True)
            place = lane - before
            label = jnp.where(mine, local + 1, 0)
            gates = gates_t[pl.ds(first, PLANE), :]
            table = jnp.full((PLANE, LANE), tok_dev, jnp.int32)
            for slot in range(MOST):
                found = jnp.sum(jnp.where(place == slot, label, 0), axis=1, keepdims=True)
                token = found - 1
                mix_t[pl.ds(pl.multiple_of(plane * PLANE * MOST, PLANE) + slot * PLANE, PLANE), :] = (
                    jnp.where(token_lane == token, gates, 0.0)
                )
                token = jnp.where(found > 0, token, tok_dev)
                table = jnp.where(slot_lane == slot, token, table)
            slots_v[plane] = table
            pltpu.make_async_copy(slots_v.at[plane], slots_s.at[plane], slot_sem).start()
            pltpu.make_async_copy(slots_v.at[plane], slots_s.at[plane], slot_sem).wait()
            for member in range(PLANE):
                for slot in range(MOST):
                    token = jnp.clip(slots_s[plane, member, slot], 0, tok_dev)
                    send_buf[plane * PLANE + member, slot] = token_tiles[token]
            send_plane(plane, row_copy, own_rows)

    mix[...] = mix_t[...].T.astype(jnp.bfloat16)

    for load in loads[2:]:
        load.wait()

    half = PLANE * MOST

    @pl.loop(0, steps)
    def _(step):
        pair = step_planes(step)
        for plane in pair:
            wait_plane(plane, recv_buf, row_recv, own_rows)
        to_rows(matrix, recv_buf, pair, rows, 0)
        taken = rows[...]
        block = 256
        for at in range(0, gate_w.shape[1], block):
            gate_act = jnp.dot(taken, gate_w[:, at : at + block], preferred_element_type=jnp.float32)
            up_act = jnp.dot(taken, up_w[:, at : at + block], preferred_element_type=jnp.float32)
            hidden[:, at : at + block] = (
                gate_act / (1.0 + jnp.exp(-gate_act)) * up_act
            ).astype(jnp.bfloat16)
        held = hidden[...]
        for at in range(0, width, block):
            result_rows[:, at : at + block] = jnp.dot(
                held, down_w[:, at : at + block], preferred_element_type=jnp.float32
            ).astype(jnp.bfloat16)
        for pack in range(2 * half // (2 * SUB)):
            tiles = to_tiles(matrix, result_rows, pack * 2 * SUB)
            for index, tile in enumerate(tiles):
                row = pack * 2 * SUB + index
                plane = pair[row // half]
                slot, member = divmod(row % half, PLANE)
                result_buf[plane * PLANE + member, slot] = tile
        for plane in pair:
            send_plane(plane, result_copy, own_results)

    @pl.loop(0, steps)
    def _(step):
        for plane in step_planes(step):
            wait_plane(plane, return_buf, result_recv, own_results)
            to_rows(
                matrix, return_buf, (plane,), return_rows, pl.multiple_of(plane * half, SUB)
            )

    weights = mix[...]
    for at in range(0, width, 256):
        out_ref[:, at : at + 256] = jnp.dot(
            weights, return_rows[:, at : at + 256], preferred_element_type=jnp.float32
        ).astype(jnp.bfloat16)

    def drain(buffer, semaphore):
        part = buffer.at[pl.ds(0, n - 1)]
        pltpu.make_async_copy(part, part, semaphore).wait()

    drain(all_picks, pick_send)
    drain(send_buf, row_send)
    drain(result_buf, result_send)


def layer(n, tokens, router, w_gate, w_up, w_down, picks):
    tok_dev, width = tokens.shape
    hidden_width = w_gate.shape[2]
    capacity = picks.shape[1]
    planes = n // PLANE
    vmem = pl.BlockSpec(memory_space=pltpu.VMEM)
    anywhere = pl.BlockSpec(memory_space=pl.ANY)
    block = (n, MOST, SUB, LANE)
    bf16 = jnp.bfloat16
    group = 2 * PLANE * MOST
    return pl.pallas_call(
        functools.partial(kernel, n),
        out_shape=jax.ShapeDtypeStruct((tok_dev, width), bf16),
        in_specs=[anywhere] * 5 + [vmem],
        out_specs=vmem,
        scratch_shapes=[
            pltpu.VMEM((tok_dev, width), bf16),
            pltpu.VMEM(router.shape, bf16),
            pltpu.VMEM((width, hidden_width), bf16),
            pltpu.VMEM((width, hidden_width), bf16),
            pltpu.VMEM((hidden_width, width), bf16),
            pltpu.VMEM((tok_dev + 1, SUB, LANE), bf16),
            pltpu.VMEM((n, tok_dev), jnp.float32),
            pltpu.VMEM((n, 1, capacity), jnp.int32),
            pltpu.VMEM((planes, PLANE, LANE), jnp.int32),
            pltpu.SMEM((planes, PLANE, LANE), jnp.int32),
            pltpu.VMEM((n * MOST, tok_dev), jnp.float32),
            pltpu.VMEM((tok_dev, n * MOST), bf16),
            pltpu.VMEM(block, bf16),
            pltpu.VMEM(block, bf16),
            pltpu.VMEM((group, width), bf16),
            pltpu.VMEM((group, hidden_width), bf16),
            pltpu.VMEM((group, width), bf16),
            pltpu.VMEM(block, bf16),
            pltpu.VMEM(block, bf16),
            pltpu.VMEM((n * MOST, width), bf16),
            pltpu.SemaphoreType.DMA((5,)),
            pltpu.SemaphoreType.DMA,
            pltpu.SemaphoreType.DMA((2,)),
            pltpu.SemaphoreType.DMA,
            pltpu.SemaphoreType.DMA((planes,)),
            pltpu.SemaphoreType.DMA,
            pltpu.SemaphoreType.DMA((planes,)),
            pltpu.SemaphoreType.DMA,
            pltpu.SemaphoreType.DMA((planes,)),
        ],
        compiler_params=pltpu.CompilerParams(collective_id=0, has_side_effects=True),
    )(tokens, router, w_gate, w_up, w_down, picks)


def solution(mesh):
    n = mesh.shape["dp"]
    return jax.shard_map(
        functools.partial(layer, n),
        mesh=mesh,
        in_specs=(
            P(("rep", "dp"), None),
            P("rep", None),
            P("dp", None, None),
            P("dp", None, None),
            P("dp", None, None),
            P(("rep", "dp"), None),
        ),
        out_specs=P(("rep", "dp"), None),
        check_vma=False,
    )
```

time: 190 us -> 92.7 us (0.49)
  waiting for transfers between devices: 94.8 us -> 0 us
  Pallas kernels: 0 us -> 87.1 us
  starting transfers between devices: 36.9 us -> 0 us
  local copies, waits for them, and re-layouts: 32.6 us -> 4.26 us
  matrix products: 16.4 us -> 0 us
  other arithmetic: 6.72 us -> 0 us
    all_to_all x4 -> x0, waiting for transfers between devices: 94.8 us -> none  [the longest x1 48.3 us: body(): lax.all_to_all(expert_out.reshape(sources, MOST, width), 'dp', split_axis...]
    pallas_call x0 -> x1, Pallas kernels: none -> 87.1 us  [layer(): pl.pallas_call(functools.partial(kernel, n), out_shape=jax.ShapeDtypeStru...]
    all_to_all x4 -> x0, starting transfers between devices: 36.9 us -> none  [the longest x1 11.8 us: body(): lax.all_to_all(to_owner, 'dp', split_axis=0, concat_axis=0, tiled=True)]
    gather x6 -> x0, local copies, waits for them, and re-layouts: 16.6 us -> none  [the longest x2 10.1 us: body(): tokens[safe_index]]
    dot_general x4 -> x0, matrix products: 16.4 us -> none  [the longest x1 6.88 us: feed_forward(): jnp.dot(hidden, down_w, preferred_element_type=jnp.float32)]
    reshape x3 -> x0, local copies, waits for them, and re-layouts: 11.1 us -> none  [the longest x1 3.7 us: body(): buffer_rows = received.reshape(sources * MOST, width)]
    select_n x6 -> x0, other arithmetic: 4.79 us -> none  [the longest x1 3.14 us: body(): jnp.where(live_slot[:, :, None], tokens[safe_index], jnp.zeros((), tokens...]
    unnamed x8 -> x2, local copies, waits for them, and re-layouts: 0.65 us -> 4.26 us
  transfers between devices with their start and end apart: 4 -> 0, of which waited for: 3 -> 0; matrix products, arithmetic and copies ran while one was open for 13% -> 0% of each run, Pallas kernels for 0% -> 0%
where the time goes in v1:
time: 92.7 us; the launch traced here: 91.4 us
  Pallas kernels  87.1 us (94%)
  local copies, waits for them, and re-layouts  4.26 us (5%)
    pallas_call x1, Pallas kernels, layer(): pl.pallas_call(functools.partial(kernel, n), out_shape=jax.ShapeDtypeStru...  87.1 us
    unnamed x2, local copies, waits for them, and re-layouts  4.26 us

profile of v1, /device:TPU:55, one launch (start us, length us, event | category | flops | bytes accessed | tf_op | source)
XLA Modules:
  0.0 91.4 jit_solution(15840418234861373059)
XLA Ops:
  0.0 2.0 %copy.7.router_hbm = bf16[2048,64]{1,0:T(8,128)(2,1)} copy(bf16[2048,64]{0,1:T(8,128)(2,1)} %param.7) | data formatting | bytes 524288 | tf_op args[1]
  2.0 87.1 %shard_map.64 = bf16[256,2048]{1,0:T(8,128)(2,1)} custom-call(bf16[256,2048]{1,0:T(8,128)(2,1)} %tokens_hbm.1, bf16[2048,64]{1,0:T(8,128)(2,1)} %copy.7.router_hbm, bf16[1,2048,768]{2,1,0:T(8,128)(2,1)} %gate_hbm.1, bf16[1,2048,768]{2,1,0:T(8,128)(2,1)} %up_hbm.1, bf16[1,768,2048]{2,1,0:T(8,128)(2,1)} %down_hbm.1, s32[1,256]{1,0:T(1,128)} %picks_ref.1), custom_call_target="tpu_custom_call" | custom-call | tf_op jit(solution)/shard_map/pallas_call | solution.py:331
  89.1 2.3 %copy.9 = bf16[256,2048]{1,0:T(8,128)(2,1)} copy(bf16[256,2048]{1,0:T(8,128)(2,1)} %shard_map.64) | data formatting | bytes 2097152

commit v2 on v1

--- a/solution.py
+++ b/solution.py
@@ -11,6 +11,8 @@
 PLANE = 8
 SUB, LANE = 16, 128
 MESH = pl.DeviceIdType.MESH
+GOING = ((1, 7), (2, 6), (3, 5), (4, 0))
+COMING = ((1, 7), (2, 6), (3, 5), (4, 0))
 
 
 def swap_matrix():
@@ -70,7 +72,7 @@
     gate_hbm,
     up_hbm,
     down_hbm,
-    picks_ref,
+    picks_hbm,
     out_ref,
     tokens,
     router,
@@ -106,13 +108,15 @@
     planes = n // PLANE
     my_plane = me // PLANE
     tok_dev, width = tokens.shape
-    capacity = picks_ref.shape[1]
+    capacity = picks_hbm.shape[1]
     steps = planes // 2
-
-    def step_planes(step):
-        up = step + 1
-        down = jnp.where(step == steps - 1, 0, planes - 1 - step)
-        return lax.rem(my_plane + up, planes), lax.rem(my_plane + down, planes)
+    half = PLANE * MOST
+
+    def step_planes(order, step):
+        pair = order[-1]
+        for index in range(steps - 1):
+            pair = [jnp.where(step == index, *both) for both in zip(order[index], pair)]
+        return [lax.rem(my_plane + distance, planes) for distance in pair]
 
     loads = [
         pltpu.make_async_copy(tokens_hbm, tokens, load_sem.at[0]),
@@ -121,6 +125,8 @@
         pltpu.make_async_copy(up_hbm.at[0], up_w, load_sem.at[3]),
         pltpu.make_async_copy(down_hbm.at[0], down_w, load_sem.at[4]),
     ]
+    own_picks = pltpu.make_async_copy(picks_hbm, all_picks.at[me], local_sem.at[2])
+    own_picks.start()
     for load in loads:
         load.start()
 
@@ -132,11 +138,12 @@
             barrier, inc=1, device_id={"dp": lax.rem(me + shift, n)}, device_id_type=MESH
         )
 
+    own_picks.wait()
     pl.semaphore_wait(barrier, n - 1)
 
     def pick_copy(target):
         return pltpu.make_async_remote_copy(
-            src_ref=picks_ref,
+            src_ref=all_picks.at[me],
             dst_ref=all_picks.at[me],
             send_sem=pick_send,
             recv_sem=pick_recv.at[my_plane],
@@ -146,7 +153,7 @@
 
     @pl.loop(0, steps)
     def _(step):
-        for plane in step_planes(step):
+        for plane in step_planes(GOING, step):
 
             @pl.loop(0, PLANE)
             def _(member):
@@ -156,17 +163,8 @@
                 def _():
                     pick_copy(target).start()
 
-    all_picks[me] = picks_ref[...]
-
     matrix = swap_matrix()
     loads[0].wait()
-    loads[1].wait()
-    logits = jnp.dot(tokens[...], router[...], preferred_element_type=jnp.float32)
-    logits = logits.T
-    powers = jnp.exp(logits - jnp.max(logits, axis=0, keepdims=True))
-    shares = powers / jnp.sum(powers, axis=0, keepdims=True)
-    gates_t[...] = (n * shares).astype(jnp.bfloat16).astype(jnp.float32)
-
     @pl.loop(0, tok_dev // (2 * SUB))
     def _(block):
         at = pl.multiple_of(block * 2 * SUB, 2 * SUB)
@@ -231,7 +229,7 @@
 
     @pl.loop(0, steps)
     def _(step):
-        for plane in step_planes(step):
+        for plane in step_planes(GOING, step):
             wait_plane(plane, all_picks, pick_recv, None)
             first = pl.multiple_of(plane * PLANE, PLANE)
             picked = all_picks[pl.ds(first, PLANE)].reshape(PLANE, capacity)
@@ -240,15 +238,10 @@
             before = jnp.sum((local < 0).astype(jnp.int32), axis=1, keepdims=True)
             place = lane - before
             label = jnp.where(mine, local + 1, 0)
-            gates = gates_t[pl.ds(first, PLANE), :]
             table = jnp.full((PLANE, LANE), tok_dev, jnp.int32)
             for slot in range(MOST):
                 found = jnp.sum(jnp.where(place == slot, label, 0), axis=1, keepdims=True)
-                token = found - 1
-                mix_t[pl.ds(pl.multiple_of(plane * PLANE * MOST, PLANE) + slot * PLANE, PLANE), :] = (
-                    jnp.where(token_lane == token, gates, 0.0)
-                )
-                token = jnp.where(found > 0, token, tok_dev)
+                token = jnp.where(found > 0, found - 1, tok_dev)
                 table = jnp.where(slot_lane == slot, token, table)
             slots_v[plane] = table
             pltpu.make_async_copy(slots_v.at[plane], slots_s.at[plane], slot_sem).start()
@@ -259,16 +252,32 @@
                     send_buf[plane * PLANE + member, slot] = token_tiles[token]
             send_plane(plane, row_copy, own_rows)
 
+    loads[1].wait()
+    logits = lax.dot_general(
+        router[...], tokens[...], (((1,), (1,)), ((), ())), preferred_element_type=jnp.float32
+    )
+    powers = jnp.exp(logits - jnp.max(logits, axis=0, keepdims=True))
+    shares = powers / jnp.sum(powers, axis=0, keepdims=True)
+    gates_t[...] = (n * shares).astype(jnp.bfloat16).astype(jnp.float32)
+
+    @pl.loop(0, planes)
+    def _(plane):
+        gates = gates_t[pl.ds(pl.multiple_of(plane * PLANE, PLANE), PLANE), :]
+        table = slots_v[plane]
+        for slot in range(MOST):
+            at = pl.multiple_of(plane * half + slot * PLANE, PLANE)
+            mix_t[pl.ds(at, PLANE), :] = jnp.where(
+                token_lane == table[:, slot : slot + 1], gates, 0.0
+            )
+
     mix[...] = mix_t[...].T.astype(jnp.bfloat16)
 
     for load in loads[2:]:
         load.wait()
 
-    half = PLANE * MOST
-
     @pl.loop(0, steps)
     def _(step):
-        pair = step_planes(step)
+        pair = step_planes(COMING, step)
         for plane in pair:
             wait_plane(plane, recv_buf, row_recv, own_rows)
         to_rows(matrix, recv_buf, pair, rows, 0)
@@ -297,7 +306,7 @@
 
     @pl.loop(0, steps)
     def _(step):
-        for plane in step_planes(step):
+        for plane in step_planes(COMING, step):
             wait_plane(plane, return_buf, result_recv, own_results)
             to_rows(
                 matrix, return_buf, (plane,), return_rows, pl.multiple_of(plane * half, SUB)
@@ -331,11 +340,11 @@
     return pl.pallas_call(
         functools.partial(kernel, n),
         out_shape=jax.ShapeDtypeStruct((tok_dev, width), bf16),
-        in_specs=[anywhere] * 5 + [vmem],
+        in_specs=[anywhere] * 6,
         out_specs=vmem,
         scratch_shapes=[
             pltpu.VMEM((tok_dev, width), bf16),
-            pltpu.VMEM(router.shape, bf16),
+            pltpu.VMEM(router.shape[::-1], bf16),
             pltpu.VMEM((width, hidden_width), bf16),
             pltpu.VMEM((width, hidden_width), bf16),
             pltpu.VMEM((hidden_width, width), bf16),
@@ -356,7 +365,7 @@
             pltpu.VMEM((n * MOST, width), bf16),
             pltpu.SemaphoreType.DMA((5,)),
             pltpu.SemaphoreType.DMA,
-            pltpu.SemaphoreType.DMA((2,)),
+            pltpu.SemaphoreType.DMA((3,)),
             pltpu.SemaphoreType.DMA,
             pltpu.SemaphoreType.DMA((planes,)),
             pltpu.SemaphoreType.DMA,
@@ -364,8 +373,15 @@
             pltpu.SemaphoreType.DMA,
             pltpu.SemaphoreType.DMA((planes,)),
         ],
-        compiler_params=pltpu.CompilerParams(collective_id=0, has_side_effects=True),
-    )(tokens, router, w_gate, w_up, w_down, picks)
+        compiler_params=pltpu.CompilerParams(
+            collective_id=0, has_side_effects=True, vmem_limit_bytes=32 * 2**20
+        ),
+    )(
+        *[
+            pltpu.with_memory_space_constraint(operand, pltpu.HBM)
+            for operand in (tokens, router.T, w_gate, w_up, w_down, picks)
+        ]
+    )
 
 
 def solution(mesh):

time: 92.7 us -> 87.7 us (0.946)
  local copies, waits for them, and re-layouts: 4.26 us -> 0.97 us
  Pallas kernels: 87.1 us -> 85.2 us
    unnamed x2 -> x1, local copies, waits for them, and re-layouts: 4.26 us -> 0.97 us
    pallas_call x1, Pallas kernels: 87.1 us -> 85.2 us  [layer(): pl.pallas_call(functools.partial(kernel, n), out_shape=jax.ShapeDtypeStru...]
where the time goes in v2:
time: 87.7 us; the launch traced here: 86.2 us
  Pallas kernels  85.2 us (97%)
  local copies, waits for them, and re-layouts  0.97 us (1%)
    pallas_call x1, Pallas kernels, layer(): pl.pallas_call(functools.partial(kernel, n), out_shape=jax.ShapeDtypeStru...  85.2 us

profile of v2, /device:TPU:55, one launch (start us, length us, event | category | flops | bytes accessed | tf_op | source)
XLA Modules:
  0.0 86.2 jit_solution(17976569590972806822)
XLA Ops:
  0.0 85.2 %shard_map.64 = bf16[256,2048]{1,0:T(8,128)(2,1)S(1)} custom-call(bf16[256,2048]{1,0:T(8,128)(2,1)} %tokens_hbm.1, bf16[64,2048]{1,0:T(8,128)(2,1)} %bitcast.1, bf16[1,2048,768]{2,1,0:T(8,128)(2,1)} %gate_hbm.1, bf16[1,2048,768]{2,1,0:T(8,128)(2,1)} %up_hbm.1, bf16[1,768,2048]{2,1,0:T(8,128)(2,1)} %down_hbm.1, s32[1,256]{1,0:T(1,128)} %picks_hbm.1), custom_call_target="tpu_custom_call" | custom-call | tf_op jit(solution)/shard_map/pallas_call | solution.py:340
  85.2 1.0 %copy.8 = bf16[256,2048]{1,0:T(8,128)(2,1)} copy(bf16[256,2048]{1,0:T(8,128)(2,1)S(1)} %shard_map.64) | data formatting | bytes 2097152

commit v3 on v2

--- a/solution.py
+++ b/solution.py
@@ -81,7 +81,8 @@
     down_w,
     token_tiles,
     gates_t,
-    all_picks,
+    picks,
+    chosen,
     slots_v,
     slots_s,
     mix_t,
@@ -108,9 +109,15 @@
     planes = n // PLANE
     my_plane = me // PLANE
     tok_dev, width = tokens.shape
-    capacity = picks_hbm.shape[1]
+    capacity = picks.shape[1]
     steps = planes // 2
+    my_member = lax.rem(me, PLANE)
     half = PLANE * MOST
+
+    def peer(plane, turn):
+        column = lax.rem(my_member // 2 + turn // 2, PLANE // 2)
+        core = lax.rem(my_member + turn, 2)
+        return plane * PLANE + column * 2 + core
 
     def step_planes(order, step):
         pair = order[-1]
@@ -125,9 +132,9 @@
         pltpu.make_async_copy(up_hbm.at[0], up_w, load_sem.at[3]),
         pltpu.make_async_copy(down_hbm.at[0], down_w, load_sem.at[4]),
     ]
-    own_picks = pltpu.make_async_copy(picks_hbm, all_picks.at[me], local_sem.at[2])
+    own_picks = pltpu.make_async_copy(picks_hbm, picks, local_sem.at[2])
     own_picks.start()
-    for load in loads:
+    for load in loads[:2]:
         load.start()
 
     barrier = pltpu.get_barrier_semaphore()
@@ -138,30 +145,47 @@
             barrier, inc=1, device_id={"dp": lax.rem(me + shift, n)}, device_id_type=MESH
         )
 
+    def send_picks(distance):
+        plane = lax.rem(my_plane + distance, planes)
+
+        @pl.loop(0, PLANE)
+        def _(turn):
+            target = peer(plane, turn)
+
+            @pl.when(target != me)
+            def _():
+                pltpu.make_async_remote_copy(
+                    src_ref=chosen.at[target],
+                    dst_ref=slots_s.at[me],
+                    send_sem=pick_send,
+                    recv_sem=pick_recv.at[my_plane],
+                    device_id={"dp": target},
+                    device_id_type=MESH,
+                ).start()
+
     own_picks.wait()
+    owner = lax.broadcasted_iota(jnp.int32, (n, capacity), 0)
+    lane = lax.broadcasted_iota(jnp.int32, (n, capacity), 1)
+    slot_lane = lax.broadcasted_iota(jnp.int32, (n, LANE), 1)
+    local = picks[...] - owner * tok_dev
+    before = jnp.sum((local < 0).astype(jnp.int32), axis=1, keepdims=True)
+    place = lane - before
+    label = jnp.where((local >= 0) & (local < tok_dev), local + 1, 0)
+    table = jnp.full((n, LANE), tok_dev, jnp.int32)
+    for slot in range(MOST):
+        found = jnp.sum(jnp.where(place == slot, label, 0), axis=1, keepdims=True)
+        table = jnp.where(slot_lane == slot, jnp.where(found > 0, found - 1, tok_dev), table)
+    chosen[...] = table.reshape(n, 1, LANE)
+
     pl.semaphore_wait(barrier, n - 1)
-
-    def pick_copy(target):
-        return pltpu.make_async_remote_copy(
-            src_ref=all_picks.at[me],
-            dst_ref=all_picks.at[me],
-            send_sem=pick_send,
-            recv_sem=pick_recv.at[my_plane],
-            device_id={"dp": target},
-            device_id_type=MESH,
-        )
-
-    @pl.loop(0, steps)
-    def _(step):
-        for plane in step_planes(GOING, step):
-
-            @pl.loop(0, PLANE)
-            def _(member):
-                target = plane * PLANE + member
-
-                @pl.when(target != me)
-                def _():
-                    pick_copy(target).start()
+    own_slots = pltpu.make_async_copy(chosen.at[me], slots_s.at[me], local_sem.at[2])
+    own_slots.start()
+
+    @pl.loop(0, planes)
+    def _(turn):
+        up, down = step_planes(GOING, turn // 2)
+        send_picks(jnp.where(turn % 2 == 0, up, down) - my_plane + planes)
+
 
     matrix = swap_matrix()
     loads[0].wait()
@@ -173,6 +197,8 @@
             token_tiles[at + index] = tile
 
     token_tiles[tok_dev] = jnp.zeros((SUB, LANE), jnp.bfloat16)
+    for load in loads[2:]:
+        load.start()
 
     def row_copy(target):
         return pltpu.make_async_remote_copy(
@@ -197,10 +223,10 @@
     own_rows = pltpu.make_async_copy(send_buf.at[me], recv_buf.at[me], local_sem.at[0])
     own_results = pltpu.make_async_copy(result_buf.at[me], return_buf.at[me], local_sem.at[1])
 
-    def send_plane(plane, copy, own):
+    def send_plane(plane, copy, own, turned):
         @pl.loop(0, PLANE)
-        def _(member):
-            target = plane * PLANE + member
+        def _(turn):
+            target = peer(plane, turn) if turned else plane * PLANE + turn
 
             @pl.when(target != me)
             def _():
@@ -223,35 +249,28 @@
             if own is not None:
                 own.wait()
 
-    lane = lax.broadcasted_iota(jnp.int32, (PLANE, capacity), 1)
     token_lane = lax.broadcasted_iota(jnp.int32, (PLANE, tok_dev), 1)
-    slot_lane = lax.broadcasted_iota(jnp.int32, (PLANE, LANE), 1)
-
-    @pl.loop(0, steps)
-    def _(step):
-        for plane in step_planes(GOING, step):
-            wait_plane(plane, all_picks, pick_recv, None)
-            first = pl.multiple_of(plane * PLANE, PLANE)
-            picked = all_picks[pl.ds(first, PLANE)].reshape(PLANE, capacity)
-            local = picked - me * tok_dev
-            mine = (local >= 0) & (local < tok_dev)
-            before = jnp.sum((local < 0).astype(jnp.int32), axis=1, keepdims=True)
-            place = lane - before
-            label = jnp.where(mine, local + 1, 0)
-            table = jnp.full((PLANE, LANE), tok_dev, jnp.int32)
+
+    def serve(plane):
+        wait_plane(plane, slots_s, pick_recv, own_slots)
+
+        @pl.loop(0, PLANE)
+        def _(member):
             for slot in range(MOST):
-                found = jnp.sum(jnp.where(place == slot, label, 0), axis=1, keepdims=True)
-                token = jnp.where(found > 0, found - 1, tok_dev)
-                table = jnp.where(slot_lane == slot, token, table)
-            slots_v[plane] = table
-            pltpu.make_async_copy(slots_v.at[plane], slots_s.at[plane], slot_sem).start()
-            pltpu.make_async_copy(slots_v.at[plane], slots_s.at[plane], slot_sem).wait()
-            for member in range(PLANE):
-                for slot in range(MOST):
-                    token = jnp.clip(slots_s[plane, member, slot], 0, tok_dev)
-                    send_buf[plane * PLANE + member, slot] = token_tiles[token]
-            send_plane(plane, row_copy, own_rows)
-
+                token = jnp.clip(slots_s[plane * PLANE + member, 0, slot], 0, tok_dev)
+                send_buf[plane * PLANE + member, slot] = token_tiles[token]
+
+        send_plane(plane, row_copy, own_rows, True)
+
+    @pl.loop(0, 2 * steps)
+    def _(turn):
+        step = turn // 2
+
+        up, down = step_planes(GOING, step)
+        serve(jnp.where(turn % 2 == 0, up, down))
+
+    slots_copy = pltpu.make_async_copy(slots_s, slots_v, slot_sem)
+    slots_copy.start()
     loads[1].wait()
     logits = lax.dot_general(
         router[...], tokens[...], (((1,), (1,)), ((), ())), preferred_element_type=jnp.float32
@@ -260,10 +279,12 @@
     shares = powers / jnp.sum(powers, axis=0, keepdims=True)
     gates_t[...] = (n * shares).astype(jnp.bfloat16).astype(jnp.float32)
 
+    slots_copy.wait()
+
     @pl.loop(0, planes)
     def _(plane):
         gates = gates_t[pl.ds(pl.multiple_of(plane * PLANE, PLANE), PLANE), :]
-        table = slots_v[plane]
+        table = slots_v[pl.ds(plane * PLANE, PLANE)].reshape(PLANE, LANE)
         for slot in range(MOST):
             at = pl.multiple_of(plane * half + slot * PLANE, PLANE)
             mix_t[pl.ds(at, PLANE), :] = jnp.where(
@@ -302,7 +323,7 @@
                 slot, member = divmod(row % half, PLANE)
                 result_buf[plane * PLANE + member, slot] = tile
         for plane in pair:
-            send_plane(plane, result_copy, own_results)
+            send_plane(plane, result_copy, own_results, False)
 
     @pl.loop(0, steps)
     def _(step):
@@ -322,7 +343,7 @@
         part = buffer.at[pl.ds(0, n - 1)]
         pltpu.make_async_copy(part, part, semaphore).wait()
 
-    drain(all_picks, pick_send)
+    drain(chosen, pick_send)
     drain(send_buf, row_send)
     drain(result_buf, result_send)
 
@@ -350,9 +371,10 @@
             pltpu.VMEM((hidden_width, width), bf16),
             pltpu.VMEM((tok_dev + 1, SUB, LANE), bf16),
             pltpu.VMEM((n, tok_dev), jnp.float32),
-            pltpu.VMEM((n, 1, capacity), jnp.int32),
-            pltpu.VMEM((planes, PLANE, LANE), jnp.int32),
-            pltpu.SMEM((planes, PLANE, LANE), jnp.int32),
+            pltpu.VMEM((1, capacity), jnp.int32),
+            pltpu.VMEM((n, 1, LANE), jnp.int32),
+            pltpu.VMEM((n, 1, LANE), jnp.int32),
+            pltpu.SMEM((n, 1, LANE), jnp.int32),
             pltpu.VMEM((n * MOST, tok_dev), jnp.float32),
             pltpu.VMEM((tok_dev, n * MOST), bf16),
             pltpu.VMEM(block, bf16),

time: 87.7 us -> 86.8 us (0.990); the launches traced: 86.2 us -> 86.7 us
  no operation moved by 1% of the time
where the time goes in v3:
time: 86.8 us; the launch traced here: 86.7 us
  Pallas kernels  85.8 us (99%)
  local copies, waits for them, and re-layouts  0.97 us (1%)
    pallas_call x1, Pallas kernels, layer(): pl.pallas_call(functools.partial(kernel, n), out_shape=jax.ShapeDtypeStru...  85.8 us

profile of v3, /device:TPU:55, one launch (start us, length us, event | category | flops | bytes accessed | tf_op | source)
XLA Modules:
  0.0 86.7 jit_solution(13519796084817321435)
XLA Ops:
  0.0 85.8 %shard_map.64 = bf16[256,2048]{1,0:T(8,128)(2,1)S(1)} custom-call(bf16[256,2048]{1,0:T(8,128)(2,1)} %tokens_hbm.1, bf16[64,2048]{1,0:T(8,128)(2,1)} %bitcast.1, bf16[1,2048,768]{2,1,0:T(8,128)(2,1)} %gate_hbm.1, bf16[1,2048,768]{2,1,0:T(8,128)(2,1)} %up_hbm.1, bf16[1,768,2048]{2,1,0:T(8,128)(2,1)} %down_hbm.1, s32[1,256]{1,0:T(1,128)} %picks_hbm.1), custom_call_target="tpu_custom_call" | custom-call | tf_op jit(solution)/shard_map/pallas_call | solution.py:361
  85.8 1.0 %copy.8 = bf16[256,2048]{1,0:T(8,128)(2,1)} copy(bf16[256,2048]{1,0:T(8,128)(2,1)S(1)} %shard_map.64) | data formatting | bytes 2097152

commit v4 on v3

--- a/solution.py
+++ b/solution.py
@@ -11,8 +11,8 @@
 PLANE = 8
 SUB, LANE = 16, 128
 MESH = pl.DeviceIdType.MESH
-GOING = ((1, 7), (2, 6), (3, 5), (4, 0))
-COMING = ((1, 7), (2, 6), (3, 5), (4, 0))
+GOING = ((1, 7), (4, 0), (3, 5), (2, 6))
+COMING = ((1, 7), (4, 0), (3, 5), (2, 6))
 
 
 def swap_matrix():
@@ -226,7 +226,7 @@
     def send_plane(plane, copy, own, turned):
         @pl.loop(0, PLANE)
         def _(turn):
-            target = peer(plane, turn) if turned else plane * PLANE + turn
+            target = peer(plane, turn) if turned else plane * PLANE + (turn // 2 + jnp.where(turn >= 6, -1, jnp.where(turn >= 4, 1, 0))) * 2 + turn % 2
 
             @pl.when(target != me)
             def _():

time: 86.8 us -> 86.4 us (level); the launches traced: 86.7 us -> 85.2 us
  Pallas kernels: 85.8 us -> 84.3 us
    pallas_call x1, Pallas kernels: 85.8 us -> 84.3 us  [layer(): pl.pallas_call(functools.partial(kernel, n), out_shape=jax.ShapeDtypeStru...]
where the time goes in v4:
time: 86.4 us; the launch traced here: 85.2 us
  Pallas kernels  84.3 us (98%)
  local copies, waits for them, and re-layouts  0.97 us (1%)
    pallas_call x1, Pallas kernels, layer(): pl.pallas_call(functools.partial(kernel, n), out_shape=jax.ShapeDtypeStru...  84.3 us

profile of v4, /device:TPU:55, one launch (start us, length us, event | category | flops | bytes accessed | tf_op | source)
XLA Modules:
  0.0 85.2 jit_solution(16620116341592089668)
XLA Ops:
  0.0 84.3 %shard_map.64 = bf16[256,2048]{1,0:T(8,128)(2,1)S(1)} custom-call(bf16[256,2048]{1,0:T(8,128)(2,1)} %tokens_hbm.1, bf16[64,2048]{1,0:T(8,128)(2,1)} %bitcast.1, bf16[1,2048,768]{2,1,0:T(8,128)(2,1)} %gate_hbm.1, bf16[1,2048,768]{2,1,0:T(8,128)(2,1)} %up_hbm.1, bf16[1,768,2048]{2,1,0:T(8,128)(2,1)} %down_hbm.1, s32[1,256]{1,0:T(1,128)} %picks_hbm.1), custom_call_target="tpu_custom_call" | custom-call | tf_op jit(solution)/shard_map/pallas_call | solution.py:361
  84.3 1.0 %copy.8 = bf16[256,2048]{1,0:T(8,128)(2,1)} copy(bf16[256,2048]{1,0:T(8,128)(2,1)S(1)} %shard_map.64) | data formatting | bytes 2097152

commit v5 on v4

--- a/solution.py
+++ b/solution.py
@@ -7,6 +7,7 @@
 from jax.experimental.pallas import tpu as pltpu
 from jax.sharding import PartitionSpec as P
 
+BLOCK = 512
 MOST = 6
 PLANE = 8
 SUB, LANE = 16, 128
@@ -73,7 +74,8 @@
     up_hbm,
     down_hbm,
     picks_hbm,
-    out_ref,
+    return_rows,
+    mix,
     tokens,
     router,
     gate_w,
@@ -86,7 +88,6 @@
     slots_v,
     slots_s,
     mix_t,
-    mix,
     send_buf,
     recv_buf,
     rows,
@@ -94,7 +95,6 @@
     result_rows,
     result_buf,
     return_buf,
-    return_rows,
     load_sem,
     slot_sem,
     local_sem,
@@ -333,12 +333,6 @@
                 matrix, return_buf, (plane,), return_rows, pl.multiple_of(plane * half, SUB)
             )
 
-    weights = mix[...]
-    for at in range(0, width, 256):
-        out_ref[:, at : at + 256] = jnp.dot(
-            weights, return_rows[:, at : at + 256], preferred_element_type=jnp.float32
-        ).astype(jnp.bfloat16)
-
     def drain(buffer, semaphore):
         part = buffer.at[pl.ds(0, n - 1)]
         pltpu.make_async_copy(part, part, semaphore).wait()
@@ -346,6 +340,24 @@
     drain(chosen, pick_send)
     drain(send_buf, row_send)
     drain(result_buf, result_send)
+
+
+def add_up(weights_ref, returned, out_hbm, held, semaphores):
+    weights = weights_ref[...]
+    copies = []
+    for at in range(0, held.shape[1], BLOCK):
+        columns = pl.ds(at, BLOCK)
+        held[:, columns] = jnp.dot(
+            weights, returned[:, columns], preferred_element_type=jnp.float32
+        ).astype(jnp.bfloat16)
+        copies.append(
+            pltpu.make_async_copy(
+                held.at[:, columns], out_hbm.at[:, columns], semaphores.at[at // BLOCK]
+            )
+        )
+        copies[-1].start()
+    for copy in copies:
+        copy.wait()
 
 
 def layer(n, tokens, router, w_gate, w_up, w_down, picks):
@@ -358,11 +370,14 @@
     block = (n, MOST, SUB, LANE)
     bf16 = jnp.bfloat16
     group = 2 * PLANE * MOST
-    return pl.pallas_call(
+    returned, weights = pl.pallas_call(
         functools.partial(kernel, n),
-        out_shape=jax.ShapeDtypeStruct((tok_dev, width), bf16),
+        out_shape=(
+            jax.ShapeDtypeStruct((n * MOST, width), bf16),
+            jax.ShapeDtypeStruct((tok_dev, n * MOST), bf16),
+        ),
         in_specs=[anywhere] * 6,
-        out_specs=vmem,
+        out_specs=(vmem, vmem),
         scratch_shapes=[
             pltpu.VMEM((tok_dev, width), bf16),
             pltpu.VMEM(router.shape[::-1], bf16),
@@ -376,7 +391,6 @@
             pltpu.VMEM((n, 1, LANE), jnp.int32),
             pltpu.SMEM((n, 1, LANE), jnp.int32),
             pltpu.VMEM((n * MOST, tok_dev), jnp.float32),
-            pltpu.VMEM((tok_dev, n * MOST), bf16),
             pltpu.VMEM(block, bf16),
             pltpu.VMEM(block, bf16),
             pltpu.VMEM((group, width), bf16),
@@ -384,7 +398,6 @@
             pltpu.VMEM((group, width), bf16),
             pltpu.VMEM(block, bf16),
             pltpu.VMEM(block, bf16),
-            pltpu.VMEM((n * MOST, width), bf16),
             pltpu.SemaphoreType.DMA((5,)),
             pltpu.SemaphoreType.DMA,
             pltpu.SemaphoreType.DMA((3,)),
@@ -404,6 +417,17 @@
             for operand in (tokens, router.T, w_gate, w_up, w_down, picks)
         ]
     )
+    return pl.pallas_call(
+        add_up,
+        out_shape=jax.ShapeDtypeStruct((tok_dev, width), bf16),
+        in_specs=[vmem, vmem],
+        out_specs=pl.BlockSpec(memory_space=pltpu.HBM),
+        scratch_shapes=[
+            pltpu.VMEM((tok_dev, width), bf16),
+            pltpu.SemaphoreType.DMA((width // BLOCK,)),
+        ],
+        compiler_params=pltpu.CompilerParams(vmem_limit_bytes=8 * 2**20),
+    )(weights, returned)
 
 
 def solution(mesh):

time: 86.4 us -> 86.2 us (level)
  local copies, waits for them, and re-layouts: 0.97 us -> 0 us
    unnamed x1 -> x0, local copies, waits for them, and re-layouts: 0.97 us -> none
    pallas_call x1 -> x2, Pallas kernels: 84.3 us -> 85 us  [the longest x1 83.6 us: layer(): pl.pallas_call(functools.partial(kernel, n), out_shape=(jax.ShapeDtypeStr...]
where the time goes in v5:
time: 86.2 us; the launch traced here: 85 us
  Pallas kernels  85 us (99%)
    pallas_call x1, Pallas kernels, layer(): pl.pallas_call(functools.partial(kernel, n), out_shape=(jax.ShapeDtypeStr...  83.6 us

profile of v5, /device:TPU:55, one launch (start us, length us, event | category | flops | bytes accessed | tf_op | source)
XLA Modules:
  0.0 85.0 jit_solution(17195793236463938452)
XLA Ops:
  0.0 83.6 %shard_map.64 = (bf16[384,2048]{1,0:T(8,128)(2,1)S(1)}, bf16[256,384]{1,0:T(8,128)(2,1)S(1)}) custom-call(bf16[256,2048]{1,0:T(8,128)(2,1)} %tokens_hbm.1, bf16[64,2048]{1,0:T(8,128)(2,1)} %bitcast.1, bf16[1,2048,768]{2,1,0:T(8,128)(2,1)} %gate_hbm.1, bf16[1,2048,768]{2,1,0:T(8,128)(2,1)} %up_hbm.1, bf16[1,768,2048]{2,1,0:T(8,128)(2,1)} %down_hbm.1, ...), custom_call_target="tpu_custom_call" | custom-call | tf_op jit(solution)/shard_map/pallas_call | solution.py:373
  83.6 1.5 %shard_map.65 = bf16[256,2048]{1,0:T(8,128)(2,1)} custom-call(bf16[256,384]{1,0:T(8,128)(2,1)S(1)} %get-tuple-element.7.weights_ref, bf16[384,2048]{1,0:T(8,128)(2,1)S(1)} %get-tuple-element.8.returned), custom_call_target="tpu_custom_call" | custom-call | tf_op jit(solution)/shard_map/pallas_call | solution.py:420

commit v6 on v5

--- a/solution.py
+++ b/solution.py
@@ -7,13 +7,13 @@
 from jax.experimental.pallas import tpu as pltpu
 from jax.sharding import PartitionSpec as P
 
-BLOCK = 512
+BLOCK = 256
 MOST = 6
 PLANE = 8
 SUB, LANE = 16, 128
 MESH = pl.DeviceIdType.MESH
-GOING = ((1, 7), (4, 0), (3, 5), (2, 6))
-COMING = ((1, 7), (4, 0), (3, 5), (2, 6))
+GOING = ((1, 7), (3, 5), (4, 0), (2, 6))
+COMING = ((1, 7), (3, 5), (4, 0), (2, 6))
 
 
 def swap_matrix():

time: 86.2 us -> 85.8 us (level)
  no operation moved by 1% of the time
where the time goes in v6:
time: 85.8 us; the launch traced here: 85.1 us
  Pallas kernels  85.1 us (99%)
    pallas_call x1, Pallas kernels, layer(): pl.pallas_call(functools.partial(kernel, n), out_shape=(jax.ShapeDtypeStr...  83.5 us

profile of v6, /device:TPU:55, one launch (start us, length us, event | category | flops | bytes accessed | tf_op | source)
XLA Modules:
  0.0 85.1 jit_solution(9260664484423449225)
XLA Ops:
  0.0 83.5 %shard_map.64 = (bf16[384,2048]{1,0:T(8,128)(2,1)S(1)}, bf16[256,384]{1,0:T(8,128)(2,1)S(1)}) custom-call(bf16[256,2048]{1,0:T(8,128)(2,1)} %tokens_hbm.1, bf16[64,2048]{1,0:T(8,128)(2,1)} %bitcast.1, bf16[1,2048,768]{2,1,0:T(8,128)(2,1)} %gate_hbm.1, bf16[1,2048,768]{2,1,0:T(8,128)(2,1)} %up_hbm.1, bf16[1,768,2048]{2,1,0:T(8,128)(2,1)} %down_hbm.1, ...), custom_call_target="tpu_custom_call" | custom-call | tf_op jit(solution)/shard_map/pallas_call | solution.py:373
  83.6 1.5 %shard_map.65 = bf16[256,2048]{1,0:T(8,128)(2,1)} custom-call(bf16[256,384]{1,0:T(8,128)(2,1)S(1)} %get-tuple-element.7.weights_ref, bf16[384,2048]{1,0:T(8,128)(2,1)S(1)} %get-tuple-element.8.returned), custom_call_target="tpu_custom_call" | custom-call | tf_op jit(solution)/shard_map/pallas_call | solution.py:420
